TPU v7x, 256 devices: a whole 4x4x8 slice. The times are simulated.
256 devices in a mesh: gx: 16 (over x_hi, y, core), vert: 16 (over z, x_lo).
Axes of the slice: x: 4 (x_hi: 2, x_lo: 2; x = x_hi * 2 + x_lo), y: 4, z: 8, core: 2. Of those that a mesh axis runs over, the one named last changes fastest.
Arguments:
- dist: float32 [13824, 64, 256], P('vert', 'gx'), as said below
- offset: int32 [13824], P('vert'), may hold values from -6 to 6, as said below
- fraction: float32 [13824], P('vert'), may hold values from 0 to 1
- cross_velocity: float32 [2, 13824], P(None, 'vert'), may hold values from -4 to 4
- relax: float32 [64, 256], P('gx'), may hold values from 0.3 to 0.9
Outputs:
- updated: float32 [13824, 64, 256], P('vert', 'gx')
Inputs may be any that keep to these rules, and one draw needn't show every extreme that they name: `offset`: each value from -6 to 6 inclusive; both ends are taken by some velocity. `dist`: Positive.
All inputs are finite; a program needn't handle non-finite values.
Results may differ from a plain program's by a relative error of at most 0.0003.
Values sent between devices are 32-bit elements; how exact they have to be, the bound alone decides.
No kernel may reach another device: no remote copies, remote signals or barrier semaphores. Data moves between devices by JAX's collectives and lax.ppermute only.
A program may use at most 64 MiB of HBM per device.

v0:
```python
import jax
import jax.numpy as jnp
from jax import lax
from jax.sharding import Mesh
from jax.sharding import PartitionSpec as P

MAXS = 6
GX = ("gx_0", "gx_1", "gx_2")


def cut_along(array, dim, size):
    before, after = (array.shape[:dim], array.shape[dim + 1 :])
    return jnp.moveaxis(array.reshape(*before, size, -1, *after), dim, 0)


def laid_out(parts, dim):
    parts = jnp.moveaxis(parts, 0, dim)
    lengths = parts.shape
    return parts.reshape(*lengths[:dim], lengths[dim] * lengths[dim + 1], *lengths[dim + 2 :])


def turned_blocks(parts, axes, sequence):
    lengths = [lax.axis_size(a) for a in axes]
    parts = parts.reshape(*lengths, *parts.shape[1:])
    for k in sequence:
        parts = lax.all_to_all(parts, axes[k], split_axis=k, concat_axis=k, tiled=True)
    return parts.reshape(-1, *parts.shape[len(axes) :])


def exchange_by_chip(array, groups, sequence, split_dim, concat_dim):
    size = lax.axis_size(groups[0]) * lax.axis_size(groups[1])
    parts = cut_along(array, split_dim, size)
    return laid_out(turned_blocks(parts, groups, sequence), concat_dim)


def sent_to_all(array, axis):
    copies = jnp.broadcast_to(array, (lax.axis_size(axis), *array.shape))
    return lax.all_to_all(copies, axis, split_axis=0, concat_axis=0, tiled=True)


def of_everyone(array, axis):
    return sent_to_all(array, axis).sum(axis=0)


def stencil_matrix(offset, fraction, row_count, col_count):
    position = 1.0 - fraction
    weights = jnp.stack(
        [
            -position * (position - 1.0) * (position - 2.0) / 6.0,
            (position + 1.0) * (position - 1.0) * (position - 2.0) / 2.0,
            -(position + 1.0) * position * (position - 2.0) / 2.0,
            (position + 1.0) * position * (position - 1.0) / 6.0,
        ],
        axis=1,
    )
    row_index = jnp.arange(row_count, dtype=jnp.int32)
    tap_index = jnp.arange(4, dtype=jnp.int32)
    target = jnp.mod(
        row_index[None, :, None] - offset[:, None, None] - 2 + tap_index[None, None, :], col_count
    )
    onehot = (target[..., None] == jnp.arange(col_count, dtype=jnp.int32)).astype(weights.dtype)
    return jnp.einsum("vrjc,vj->vrc", onehot, weights, precision=lax.Precision.HIGHEST)


def velocities(offset, fraction, cross_velocity):
    along = (offset.astype(fraction.dtype) + fraction) * (3.0 / MAXS)
    return (along, cross_velocity[0], cross_velocity[1])


def cell_state(sums):
    density = sums[0]
    mean_x = sums[1] / density
    mean_y = sums[2] / density
    mean_z = sums[3] / density
    temper = (sums[4] / density - (mean_x * mean_x + mean_y * mean_y + mean_z * mean_z)) / 3.0
    return jnp.stack([density, mean_x, mean_y, mean_z, temper])


def equilibrium(vel_x, vel_y, vel_z, state):
    diff_x = vel_x[:, None, None] - state[1]
    diff_y = vel_y[:, None, None] - state[2]
    diff_z = vel_z[:, None, None] - state[3]
    return jnp.exp(-(diff_x * diff_x + diff_y * diff_y + diff_z * diff_z) / (2.0 * state[4]))


def per_device(dist, offset, fraction, cross_velocity, relax):
    local_vel, local_cells, window = dist.shape
    group_count = lax.axis_size(GX)
    subset = local_vel // group_count
    start = lax.axis_index(GX) * subset
    lines = lax.all_to_all(dist, GX, split_axis=0, concat_axis=1, tiled=True)
    line_cells = local_cells * group_count
    shift_part = lax.dynamic_slice_in_dim(offset, start, subset)
    frac_part = lax.dynamic_slice_in_dim(fraction, start, subset)
    matrix = stencil_matrix(shift_part, frac_part, line_cells, line_cells)
    moved = jnp.einsum("vrc,vcn->vrn", matrix, lines, precision=lax.Precision.HIGHEST)
    shifted = exchange_by_chip(moved, (("gx_0", "gx_1"), "gx_2"), (1, 0), 1, 0)
    vel_x, vel_y, vel_z = velocities(offset, fraction, cross_velocity)
    coeffs = jnp.stack(
        [jnp.ones_like(vel_x), vel_x, vel_y, vel_z, vel_x * vel_x + vel_y * vel_y + vel_z * vel_z]
    )
    partial_sums = jnp.einsum("mv,vxn->mxn", coeffs, shifted, precision=lax.Precision.HIGHEST)
    state = cell_state(of_everyone(partial_sums, "vert"))
    weight = equilibrium(vel_x, vel_y, vel_z, state)
    total = of_everyone(jnp.sum(weight, axis=0), "vert")
    return shifted + relax[None] * (state[0] * weight / total - shifted)


def solution(mesh):
    torus = Mesh(
        mesh.devices.reshape(2, 4, 2, mesh.shape["vert"]), ("gx_0", "gx_1", "gx_2", "vert")
    )
    placed = (P("vert", GX, None), P("vert"), P("vert"), P(None, "vert"), P(GX, None))
    return jax.shard_map(
        per_device, mesh=torus, in_specs=placed, out_specs=P("vert", GX, None), check_vma=False
    )
```

profile of v0, /device:TPU:4, one launch (start us, length us, event | category | flops | bytes accessed | tf_op | source)
XLA Modules:
  0.0 182.1 jit_solution(566256399795120523)
XLA Ops:
  0.0 7.5 %all-to-all-start = ((f32[864,4,256]{2,1,0:T(4,128)}), f32[864,4,256]{2,1,0:T(4,128)S(1)}, u32[]{:S(2)}, u32[]{:S(2)}) async-start(f32[864,4,256]{2,1,0:T(4,128)} %param.5), calls=%async_computation | async-start | bytes 7077888 | tf_op jit(solution)/shard_map/all_to_all | solution.py:91
  7.5 0.8 multiply_bitcast_fusion.4
  8.2 0.7 copy.44
  8.9 0.8 dynamic_slice.6
  9.7 0.1 subtract_add_fusion
  9.8 0.7 add_select_fusion
  10.5 2.7 %copy.34 = s32[54,64,4]{2,1,0:T(8,128)} copy(s32[54,64,4]{1,2,0:T(4,128)} %add_select_fusion) | data formatting | bytes 110592 | tf_op jit(solution)/shard_map/jit(remainder)/select_n | solution.py:58
  13.2 12.8 %fusion = f32[54,1,64,64]{3,1,2,0:T(1,128)} fusion(f32[54,4,1,1]{1,2,3,0:T(1,128)} %copy.44, s32[54,64,4]{2,1,0:T(8,128)} %copy.34), kind=kOutput, calls=%fused_computation.1 | convolution fusion | flops 11501568 | bytes 940896 | tf_op jit(solution)/shard_map/vrjc,vj->vrc/dot_general | solution.py:62
  26.0 24.0 %all-to-all-done = f32[864,4,256]{2,1,0:T(4,128)S(1)} async-done(((f32[864,4,256]{2,1,0:T(4,128)}), f32[864,4,256]{2,1,0:T(4,128)S(1)}, u32[]{:S(2)}, u32[]{:S(2)}) %all-to-all-start) | async-done | bytes 3538976 | tf_op jit(solution)/shard_map/all_to_all | solution.py:91
  50.0 2.8 %copy.59 = f32[16,54,4,256]{3,2,0,1:T(4,128)} copy(f32[16,54,4,256]{3,2,1,0:T(4,128)S(1)} %bitcast.42) | data formatting | bytes 7077888 | tf_op jit(solution)/shard_map/all_to_all | solution.py:91
  52.8 3.4 %all_to_all.28 = f32[54,64,256]{2,1,0:T(8,128)S(1)} reshape(f32[54,16,4,256]{3,2,1,0:T(4,128)} %bitcast.43) | data formatting | bytes 7077888 | tf_op jit(solution)/shard_map/all_to_all | solution.py:91
  56.2 4.9 %fusion.17 = f32[54,64,256]{2,1,0:T(8,128)S(1)} fusion(f32[54,64,64]{2,1,0:T(8,128)} %bitcast.44, f32[54,64,256]{2,1,0:T(8,128)S(1)} %all_to_all.28), kind=kOutput, calls=%fused_computation.45 | convolution fusion | flops 679477248 | bytes 7962624 | tf_op jit(solution)/shard_map/vrc,vcn->vrn/dot_general | solution.py:96
  61.1 2.1 %copy.46 = f32[54,64,256]{2,0,1:T(8,128)S(1)} copy(f32[54,64,256]{2,1,0:T(8,128)S(1)} %fusion.17) | data formatting | bytes 7077888 | tf_op jit(solution)/shard_map/reshape | solution.py:13
  63.1 2.1 %copy.37 = f32[8,2,54,4,256]{4,0,3,2,1:T(8,128)S(1)} copy(f32[8,2,54,4,256]{4,2,3,1,0:T(8,128)S(1)} %bitcast.41) | data formatting | bytes 7077888 | tf_op jit(solution)/shard_map/reshape | solution.py:24
  65.2 6.6 %all_to_all.38 = f32[8,2,54,4,256]{4,0,3,2,1:T(8,128)S(1)} all-to-all(f32[8,2,54,4,256]{4,0,3,2,1:T(8,128)S(1)} %copy.37), channel_id=1, replica_groups=mesh['gx_0'=2,'gx_1'=4,'gx_2'=2,'vert'=16] {'gx_2'}, dimensions={1} | all-to-all | bytes 7077888 | tf_op jit(solution)/shard_map/all_to_all | solution.py:26
  71.8 3.2 %copy.38 = f32[8,2,54,4,256]{4,3,2,1,0:T(4,128)} copy(f32[8,2,54,4,256]{4,0,3,2,1:T(8,128)S(1)} %all_to_all.38) | data formatting | bytes 7077888 | tf_op jit(solution)/shard_map/all_to_all | solution.py:26
  74.9 0.0 copy-start
  74.9 15.8 %all-to-all-start.2 = ((f32[8,2,54,4,256]{4,3,2,1,0:T(4,128)}), f32[8,2,54,4,256]{4,3,2,1,0:T(4,128)S(1)}, u32[]{:S(2)}, u32[]{:S(2)}) async-start(f32[8,2,54,4,256]{4,3,2,1,0:T(4,128)} %copy.38), calls=%async_computation.2 | async-start | bytes 7077888 | tf_op jit(solution)/shard_map/all_to_all | solution.py:26
  90.7 0.0 copy-done
  90.7 0.7 multiply_add_fusion.1
  91.4 0.6 stack.34
  92.0 0.5 pad.clone
  92.6 39.4 %all-to-all-done.2 = f32[8,2,54,4,256]{4,3,2,1,0:T(4,128)S(1)} async-done(((f32[8,2,54,4,256]{4,3,2,1,0:T(4,128)}), f32[8,2,54,4,256]{4,3,2,1,0:T(4,128)S(1)}, u32[]{:S(2)}, u32[]{:S(2)}) %all-to-all-start.2) | async-done | bytes 3538976 | tf_op jit(solution)/shard_map/all_to_all | solution.py:26
  131.9 2.9 %fusion.2 = f32[5,4,256]{2,0,1:T(8,128)S(1)} fusion(f32[864,4,256]{2,1,0:T(4,128)S(1)} %bitcast.39, f32[1,864]{1,0:T(1,128)} %stack.34, f32[2,864]{1,0:T(2,128)} %param.8, f32[1,864]{1,0:T(1,128)S(1)} %stack.33, f32[5]{0:T(128)} %pad.clone), kind=kOutput, calls=%fused_computation.6 | convolution fusion | flops 53097120 | bytes 3573268 | tf_op jit(solution)/shard_map/mv,vxn->mxn/dot_general | solution.py:102
  134.9 21.6 %all_to_all.39 = f32[16,5,4,256]{3,2,1,0:T(4,128)} all-to-all(f32[16,5,4,256]{3,2,1,0:T(4,128)S(1)} %broadcast_in_dim.4), channel_id=1, replica_groups=mesh['gx_0'=2,'gx_1'=4,'gx_2'=2,'vert'=16] {'vert'}, dimensions={0} | all-to-all | bytes 655360 | tf_op jit(solution)/shard_map/all_to_all | solution.py:38
  156.5 1.6 reduce_sum.27
  158.1 0.8 slice_bitcast_fusion
  158.9 0.0 copy-start.1
  158.9 0.0 copy-start.2
  158.9 0.0 copy-start.3
  158.9 0.0 copy-start.4
  158.9 0.6 copy-done.1
  159.5 1.7 fusion.4
  161.1 0.0 copy-done.2
  161.2 0.0 copy-done.3
  161.2 0.0 copy-done.4
  161.2 12.4 %all_to_all.40 = f32[16,4,256]{2,1,0:T(4,128)} all-to-all(f32[16,4,256]{2,1,0:T(4,128)S(1)} %broadcast_in_dim.5), channel_id=1, replica_groups=mesh['gx_0'=2,'gx_1'=4,'gx_2'=2,'vert'=16] {'vert'}, dimensions={0} | all-to-all | bytes 131072 | tf_op jit(solution)/shard_map/all_to_all | solution.py:38
  173.6 1.5 reduce_sum.29
  175.0 3.0 %multiply_add_fusion = f32[864,4,256]{2,0,1:T(8,128)S(1)} fusion(f32[864,4,256]{2,1,0:T(4,128)S(1)} %bitcast.40, f32[4,256]{1,0:T(4,128)} %reduce_sum.29, f32[4,256]{1,0:T(4,128)} %copy-done.4, f32[4,256]{1,0:T(4,128)} %copy-done.1, f32[864]{0:T(1024)S(1)} %get-tuple-element.6, f32[4,256]{1,0:T(4,128)} %copy-done.2, f32[864]{0:T(1024)S(1)} %get-tuple-element.5, ...), kind=kLoop, calls=%fused_computation.3 | loop fusion | flops 13271040 | bytes 7116928 | tf_op jit(solution)/shard_map/add | solution.py:106
  178.0 4.1 %copy.43 = f32[864,4,256]{2,1,0:T(4,128)} copy(f32[864,4,256]{2,0,1:T(8,128)S(1)} %multiply_add_fusion) | data formatting | bytes 7077888 | tf_op jit(solution)/shard_map/add | solution.py:106
  (7 shorter events, 0.1 us)
Async XLA Ops:
  0.0 50.0 %all-to-all-start = ((f32[864,4,256]{2,1,0:T(4,128)}), f32[864,4,256]{2,1,0:T(4,128)S(1)}, u32[]{:S(2)}, u32[]{:S(2)}) async-start(f32[864,4,256]{2,1,0:T(4,128)} %param.5), calls=%async_computation | async-start | bytes 7077888 | tf_op jit(solution)/shard_map/all_to_all | solution.py:91
  74.9 15.8 %copy-start = (f32[2,864]{1,0:T(2,128)S(1)}, f32[2,864]{1,0:T(2,128)}, u32[]{:S(2)}) copy-start(f32[2,864]{1,0:T(2,128)} %param.8) | copy-start | bytes 20740
  74.9 57.0 %all-to-all-start.2 = ((f32[8,2,54,4,256]{4,3,2,1,0:T(4,128)}), f32[8,2,54,4,256]{4,3,2,1,0:T(4,128)S(1)}, u32[]{:S(2)}, u32[]{:S(2)}) async-start(f32[8,2,54,4,256]{4,3,2,1,0:T(4,128)} %copy.38), calls=%async_computation.2 | async-start | bytes 7077888 | tf_op jit(solution)/shard_map/all_to_all | solution.py:26
  158.9 0.6 copy-start.1
  158.9 2.3 %copy-start.2 = (f32[4,256]{1,0:T(4,128)}, f32[4,256]{1,0:T(4,128)S(1)}, u32[]{:S(2)}) copy-start(f32[4,256]{1,0:T(4,128)S(1)} %get-tuple-element.13) | copy-start | bytes 12292
  158.9 2.3 %copy-start.3 = (f32[4,256]{1,0:T(4,128)}, f32[4,256]{1,0:T(4,128)S(1)}, u32[]{:S(2)}) copy-start(f32[4,256]{1,0:T(4,128)S(1)} %get-tuple-element.14) | copy-start | bytes 12292
  158.9 2.3 %copy-start.4 = (f32[4,256]{1,0:T(4,128)}, f32[4,256]{1,0:T(4,128)S(1)}, u32[]{:S(2)}) copy-start(f32[4,256]{1,0:T(4,128)S(1)} %get-tuple-element.15) | copy-start | bytes 12292
where the time goes:
time: 183 us; the launch traced here: 182 us
  waiting for transfers between devices  63.3 us (35%)
  blocking collectives  40.5 us (22%)
  local copies, waits for them, and re-layouts  23.4 us (13%)
  starting transfers between devices  23.2 us (13%)
  matrix products  20.6 us (11%)
  other arithmetic  10.8 us (6%)
    all_to_all x1, waiting for transfers between devices, turned_blocks(): lax.all_to_all(parts, axes[k], split_axis=k, concat_axis=k, tiled=True)  39.4 us
    all_to_all x2, blocking collectives, sent_to_all(): return lax.all_to_all(copies, axis, split_axis=0, concat_axis=0, tiled=True)  33.9 us
    all_to_all x1, waiting for transfers between devices, per_device(): lines = lax.all_to_all(dist, GX, split_axis=0, concat_axis=1, tiled=True)  24 us
    all_to_all x1, starting transfers between devices, turned_blocks(): lax.all_to_all(parts, axes[k], split_axis=k, concat_axis=k, tiled=True)  15.8 us
    dot_general x1, matrix products, stencil_matrix(): jnp.einsum('vrjc,vj->vrc', onehot, weights, precision=lax.Precision.HIGHEST)  12.8 us
    all_to_all x1, starting transfers between devices, per_device(): lines = lax.all_to_all(dist, GX, split_axis=0, concat_axis=1, tiled=True)  7.45 us
    all_to_all x1, blocking collectives, turned_blocks(): lax.all_to_all(parts, axes[k], split_axis=k, concat_axis=k, tiled=True)  6.58 us
    all_to_all x2, local copies, waits for them, and re-layouts, per_device(): lines = lax.all_to_all(dist, GX, split_axis=0, concat_axis=1, tiled=True)  6.18 us
  transfers between devices with their start and end apart: 2, of which 2 were waited for; matrix products, arithmetic and copies ran while one was open for 11% of the time, Pallas kernels for 0%

commit v1 on v0

--- a/solution.py
+++ b/solution.py
@@ -88,7 +88,9 @@
     group_count = lax.axis_size(GX)
     subset = local_vel // group_count
     start = lax.axis_index(GX) * subset
-    lines = lax.all_to_all(dist, GX, split_axis=0, concat_axis=1, tiled=True)
+    lines = jnp.concatenate(
+        lax.all_to_all(jnp.stack(jnp.split(dist, lax.axis_size(GX), axis=0)), GX, 0, 0), axis=1
+    )
     line_cells = local_cells * group_count
     shift_part = lax.dynamic_slice_in_dim(offset, start, subset)
     frac_part = lax.dynamic_slice_in_dim(fraction, start, subset)

time: 183 us -> 209 us (1.14)
  local copies, waits for them, and re-layouts: 23.4 us -> 49.6 us
    unnamed x10 -> x25, local copies, waits for them, and re-layouts: 0.57 us -> 25.1 us
    reshape x0 -> x2, local copies, waits for them, and re-layouts: none -> 6.18 us  [per_device(): jnp.concatenate(lax.all_to_all(jnp.stack(jnp.split(dist, lax.axis_size(GX...]
    all_to_all x2 -> x0, local copies, waits for them, and re-layouts: 6.18 us -> none  [per_device(): lines = lax.all_to_all(dist, GX, split_axis=0, concat_axis=1, tiled=True)]
  transfers between devices with their start and end apart: 2 -> 2, of which waited for: 2 -> 2; matrix products, arithmetic and copies ran while one was open for 11% -> 10% of each run, Pallas kernels for 0% -> 0%
where the time goes in v1:
time: 209 us; the launch traced here: 208 us
  waiting for transfers between devices  63.4 us (30%)
  local copies, waits for them, and re-layouts  49.6 us (24%)
  blocking collectives  40.5 us (19%)
  starting transfers between devices  23.2 us (11%)
  matrix products  20.6 us (10%)
  other arithmetic  10.8 us (5%)
    all_to_all x1, waiting for transfers between devices, turned_blocks(): lax.all_to_all(parts, axes[k], split_axis=k, concat_axis=k, tiled=True)  39.4 us
    all_to_all x2, blocking collectives, sent_to_all(): return lax.all_to_all(copies, axis, split_axis=0, concat_axis=0, tiled=True)  33.9 us
    unnamed x25, local copies, waits for them, and re-layouts  25.1 us
    all_to_all x1, waiting for transfers between devices, per_device(): lax.all_to_all(jnp.stack(jnp.split(dist, lax.axis_size(GX), axis=0)), GX,...  24 us
    all_to_all x1, starting transfers between devices, turned_blocks(): lax.all_to_all(parts, axes[k], split_axis=k, concat_axis=k, tiled=True)  15.8 us
    dot_general x1, matrix products, stencil_matrix(): jnp.einsum('vrjc,vj->vrc', onehot, weights, precision=lax.Precision.HIGHEST)  12.8 us
    all_to_all x1, starting transfers between devices, per_device(): lax.all_to_all(jnp.stack(jnp.split(dist, lax.axis_size(GX), axis=0)), GX,...  7.45 us
    all_to_all x1, blocking collectives, turned_blocks(): lax.all_to_all(parts, axes[k], split_axis=k, concat_axis=k, tiled=True)  6.58 us
  transfers between devices with their start and end apart: 2, of which 2 were waited for; matrix products, arithmetic and copies ran while one was open for 10% of the time, Pallas kernels for 0%

profile of v1, /device:TPU:4, one launch (start us, length us, event | category | flops | bytes accessed | tf_op | source)
XLA Modules:
  0.0 208.2 jit_solution(2643114164208156274)
XLA Ops:
  0.0 1.6 bitcast_dynamic-update-slice_fusion.15
  1.6 1.6 bitcast_dynamic-update-slice_fusion.14
  3.3 1.6 bitcast_dynamic-update-slice_fusion.13
  4.9 1.6 bitcast_dynamic-update-slice_fusion.12
  6.5 1.6 bitcast_dynamic-update-slice_fusion.11
  8.2 1.6 bitcast_dynamic-update-slice_fusion.10
  9.8 1.6 bitcast_dynamic-update-slice_fusion.9
  11.4 1.6 bitcast_dynamic-update-slice_fusion.8
  13.1 1.6 bitcast_dynamic-update-slice_fusion.7
  14.7 1.6 bitcast_dynamic-update-slice_fusion.6
  16.3 1.6 bitcast_dynamic-update-slice_fusion.5
  18.0 1.6 bitcast_dynamic-update-slice_fusion.4
  19.6 1.6 bitcast_dynamic-update-slice_fusion.3
  21.3 1.6 bitcast_dynamic-update-slice_fusion.2
  22.9 1.6 bitcast_dynamic-update-slice_fusion.1
  24.5 1.6 bitcast_dynamic-update-slice_fusion
  26.2 7.5 %all-to-all-start = ((f32[16,54,4,256]{3,2,1,0:T(4,128)}), f32[16,54,4,256]{3,2,1,0:T(4,128)S(1)}, u32[]{:S(2)}, u32[]{:S(2)}) async-start(f32[16,54,4,256]{3,2,1,0:T(4,128)} %bitcast_dynamic-update-slice_fusion), calls=%async_computation | async-start | bytes 7077888 | tf_op jit(solution)/shard_map/all_to_all | solution.py:92
  33.6 0.8 multiply_bitcast_fusion.4
  34.4 0.7 copy.44
  35.1 0.8 dynamic_slice.6
  35.9 0.1 subtract_add_fusion
  35.9 0.7 add_select_fusion
  36.7 2.7 %copy.34 = s32[54,64,4]{2,1,0:T(8,128)} copy(s32[54,64,4]{1,2,0:T(4,128)} %add_select_fusion) | data formatting | bytes 110592 | tf_op jit(solution)/shard_map/jit(remainder)/select_n | solution.py:58
  39.4 12.8 %fusion = f32[54,1,64,64]{3,1,2,0:T(1,128)} fusion(f32[54,4,1,1]{1,2,3,0:T(1,128)} %copy.44, s32[54,64,4]{2,1,0:T(8,128)} %copy.34), kind=kOutput, calls=%fused_computation.1 | convolution fusion | flops 11501568 | bytes 940896 | tf_op jit(solution)/shard_map/vrjc,vj->vrc/dot_general | solution.py:62
  52.1 24.0 %all-to-all-done = f32[16,54,4,256]{3,2,1,0:T(4,128)S(1)} async-done(((f32[16,54,4,256]{3,2,1,0:T(4,128)}), f32[16,54,4,256]{3,2,1,0:T(4,128)S(1)}, u32[]{:S(2)}, u32[]{:S(2)}) %all-to-all-start) | async-done | bytes 3538976 | tf_op jit(solution)/shard_map/all_to_all | solution.py:92
  76.1 2.8 %copy.35 = f32[54,16,4,256]{3,2,1,0:T(4,128)} copy(f32[54,16,4,256]{3,2,0,1:T(4,128)S(1)} %bitcast.71) | data formatting | bytes 7077888 | tf_op jit(solution)/shard_map/reshape | solution.py:91
  78.9 3.4 %reshape.59 = f32[54,64,256]{2,1,0:T(8,128)S(1)} reshape(f32[54,16,4,256]{3,2,1,0:T(4,128)} %copy.35) | data formatting | bytes 7077888 | tf_op jit(solution)/shard_map/reshape | solution.py:91
  82.3 4.9 %fusion.17 = f32[54,64,256]{2,1,0:T(8,128)S(1)} fusion(f32[54,64,64]{2,1,0:T(8,128)} %bitcast.72, f32[54,64,256]{2,1,0:T(8,128)S(1)} %reshape.59), kind=kOutput, calls=%fused_computation.60 | convolution fusion | flops 679477248 | bytes 7962624 | tf_op jit(solution)/shard_map/vrc,vcn->vrn/dot_general | solution.py:98
  87.2 2.1 copy.46
  89.3 2.1 copy.37
  91.4 6.6 %all_to_all.25 = f32[8,2,54,4,256]{4,0,3,2,1:T(8,128)S(1)} all-to-all(f32[8,2,54,4,256]{4,0,3,2,1:T(8,128)S(1)} %copy.37), channel_id=1, replica_groups=mesh['gx_0'=2,'gx_1'=4,'gx_2'=2,'vert'=16] {'gx_2'}, dimensions={1} | all-to-all | bytes 7077888 | tf_op jit(solution)/shard_map/all_to_all | solution.py:26
  97.9 3.2 %copy.38 = f32[8,2,54,4,256]{4,3,2,1,0:T(4,128)} copy(f32[8,2,54,4,256]{4,0,3,2,1:T(8,128)S(1)} %all_to_all.25) | data formatting | bytes 7077888 | tf_op jit(solution)/shard_map/all_to_all | solution.py:26
  101.1 15.8 %all-to-all-start.2 = ((f32[8,2,54,4,256]{4,3,2,1,0:T(4,128)}), f32[8,2,54,4,256]{4,3,2,1,0:T(4,128)S(1)}, u32[]{:S(2)}, u32[]{:S(2)}) async-start(f32[8,2,54,4,256]{4,3,2,1,0:T(4,128)} %copy.38), calls=%async_computation.2 | async-start | bytes 7077888 | tf_op jit(solution)/shard_map/all_to_all | solution.py:26
  116.9 0.0 copy-done
  116.9 0.7 multiply_add_fusion.1
  117.6 0.6 stack.102
  118.2 0.5 pad.clone
  118.7 39.4 %all-to-all-done.2 = f32[8,2,54,4,256]{4,3,2,1,0:T(4,128)S(1)} async-done(((f32[8,2,54,4,256]{4,3,2,1,0:T(4,128)}), f32[8,2,54,4,256]{4,3,2,1,0:T(4,128)S(1)}, u32[]{:S(2)}, u32[]{:S(2)}) %all-to-all-start.2) | async-done | bytes 3538976 | tf_op jit(solution)/shard_map/all_to_all | solution.py:26
  158.1 2.9 %fusion.2 = f32[5,4,256]{2,0,1:T(8,128)S(1)} fusion(f32[864,4,256]{2,1,0:T(4,128)S(1)} %bitcast.68, f32[1,864]{1,0:T(1,128)} %stack.102, f32[2,864]{1,0:T(2,128)} %param.8, f32[1,864]{1,0:T(1,128)S(1)} %stack.101, f32[5]{0:T(128)} %pad.clone), kind=kOutput, calls=%fused_computation.5 | convolution fusion | flops 53097120 | bytes 3573268 | tf_op jit(solution)/shard_map/mv,vxn->mxn/dot_general | solution.py:104
  161.1 21.6 %all_to_all.26 = f32[16,5,4,256]{3,2,1,0:T(4,128)} all-to-all(f32[16,5,4,256]{3,2,1,0:T(4,128)S(1)} %broadcast_in_dim.4), channel_id=1, replica_groups=mesh['gx_0'=2,'gx_1'=4,'gx_2'=2,'vert'=16] {'vert'}, dimensions={0} | all-to-all | bytes 655360 | tf_op jit(solution)/shard_map/all_to_all | solution.py:38
  182.6 1.6 reduce_sum.27
  184.3 0.8 slice_bitcast_fusion
  185.1 0.6 copy-done.1
  185.6 1.7 fusion.4
  187.4 12.4 %all_to_all.27 = f32[16,4,256]{2,1,0:T(4,128)} all-to-all(f32[16,4,256]{2,1,0:T(4,128)S(1)} %broadcast_in_dim.5), channel_id=1, replica_groups=mesh['gx_0'=2,'gx_1'=4,'gx_2'=2,'vert'=16] {'vert'}, dimensions={0} | all-to-all | bytes 131072 | tf_op jit(solution)/shard_map/all_to_all | solution.py:38
  199.7 1.5 reduce_sum.29
  201.2 3.0 %multiply_add_fusion = f32[864,4,256]{2,0,1:T(8,128)S(1)} fusion(f32[864,4,256]{2,1,0:T(4,128)S(1)} %bitcast.69, f32[4,256]{1,0:T(4,128)} %reduce_sum.29, f32[4,256]{1,0:T(4,128)} %copy-done.4, f32[4,256]{1,0:T(4,128)} %copy-done.1, f32[864]{0:T(1024)S(1)} %get-tuple-element.6, f32[4,256]{1,0:T(4,128)} %copy-done.2, f32[864]{0:T(1024)S(1)} %get-tuple-element.5, ...), kind=kLoop, calls=%fused_computation.2 | loop fusion | flops 13271040 | bytes 7116928 | tf_op jit(solution)/shard_map/add | solution.py:108
  204.1 4.1 %copy.43 = f32[864,4,256]{2,1,0:T(4,128)} copy(f32[864,4,256]{2,0,1:T(8,128)S(1)} %multiply_add_fusion) | data formatting | bytes 7077888 | tf_op jit(solution)/shard_map/add | solution.py:108
  (15 shorter events, 0.1 us)
Async XLA Ops:
  26.2 50.0 %all-to-all-start = ((f32[16,54,4,256]{3,2,1,0:T(4,128)}), f32[16,54,4,256]{3,2,1,0:T(4,128)S(1)}, u32[]{:S(2)}, u32[]{:S(2)}) async-start(f32[16,54,4,256]{3,2,1,0:T(4,128)} %bitcast_dynamic-update-slice_fusion), calls=%async_computation | async-start | bytes 7077888 | tf_op jit(solution)/shard_map/all_to_all | solution.py:92
  101.1 15.8 %copy-start = (f32[2,864]{1,0:T(2,128)S(1)}, f32[2,864]{1,0:T(2,128)}, u32[]{:S(2)}) copy-start(f32[2,864]{1,0:T(2,128)} %param.8) | copy-start | bytes 20740
  101.1 57.0 %all-to-all-start.2 = ((f32[8,2,54,4,256]{4,3,2,1,0:T(4,128)}), f32[8,2,54,4,256]{4,3,2,1,0:T(4,128)S(1)}, u32[]{:S(2)}, u32[]{:S(2)}) async-start(f32[8,2,54,4,256]{4,3,2,1,0:T(4,128)} %copy.38), calls=%async_computation.2 | async-start | bytes 7077888 | tf_op jit(solution)/shard_map/all_to_all | solution.py:26
  185.0 0.6 copy-start.1
  185.0 2.3 %copy-start.2 = (f32[4,256]{1,0:T(4,128)}, f32[4,256]{1,0:T(4,128)S(1)}, u32[]{:S(2)}) copy-start(f32[4,256]{1,0:T(4,128)S(1)} %get-tuple-element.13) | copy-start | bytes 12292
  185.0 2.3 %copy-start.3 = (f32[4,256]{1,0:T(4,128)}, f32[4,256]{1,0:T(4,128)S(1)}, u32[]{:S(2)}) copy-start(f32[4,256]{1,0:T(4,128)S(1)} %get-tuple-element.14) | copy-start | bytes 12292
  185.0 2.3 %copy-start.4 = (f32[4,256]{1,0:T(4,128)}, f32[4,256]{1,0:T(4,128)S(1)}, u32[]{:S(2)}) copy-start(f32[4,256]{1,0:T(4,128)S(1)} %get-tuple-element.15) | copy-start | bytes 12292
